TPU v7x, 32 devices: a whole 2x2x4 slice. The times are simulated.
32 devices in a mesh: ens: 4 (over y, x), lon: 8 (over z, core).
Axes of the slice: x: 2, y: 2, z: 4, core: 2. Of those that a mesh axis runs over, the one named last changes fastest.
Arguments:
- control: float32 [8, 1024, 512], P('ens', None, 'lon'), may hold values from -6 to 6
- residual: float32 [8, 1024, 512], P('ens', None, 'lon'), may hold values from -6 to 6
- direction: float32 [8, 1024, 512], P('ens', None, 'lon'), may hold values from -6 to 6
- ens_perturb: bfloat16 [8, 3, 1024, 512], P('ens', None, None, 'lon'), may hold values from -1.5 to 1.5
- localize: float32 [1024, 1024], replicated, may hold values from -0.5 to 1.5
- obs_cell: int32 [32768], P('lon'), may hold values from 0 to 65535
- obs_slot: int32 [32768], P('lon'), may hold values from 0 to 3
- obs_weight: float32 [32768], P('lon'), may hold values from 0.5 to 4
Outputs:
- control_new: float32 [8, 1024, 512], P('ens', None, 'lon')
- residual_new: float32 [8, 1024, 512], P('ens', None, 'lon')
- direction_new: float32 [8, 1024, 512], P('ens', None, 'lon')
Inputs may be any that keep to these rules, and one draw needn't show every extreme that they name: `obs_cell`: row-major cell within the entry's own longitude tile: row times 64 plus column. `obs_slot`: slot n < 3 observes the height after model step n + 1; slot 3 marks a padding entry that observes nothing.
All inputs are finite; a program needn't handle non-finite values.
Results may differ from a plain program's by a relative error of at most 0.0003.
Values sent between devices are 32-bit elements; how exact they have to be, the bound alone decides.
A program may use at most 64 MiB of HBM per device.

v0:
```python
import jax
import jax.numpy as jnp
from jax import lax
from jax.sharding import PartitionSpec as P

STEPS = 3
wave_speed = 0.35
rotation = 0.2


def extended(block, sides, width):
    for axis, dim in sides:
        count = lax.axis_size(axis)
        forward = [(i, i + 1) for i in range(count - 1)]
        forward.append((count - 1, 0))
        backward = [(target, source) for source, target in forward]
        low = lax.ppermute(
            lax.slice_in_dim(block, block.shape[dim] - width, None, axis=dim), axis, forward
        )
        high = lax.ppermute(lax.slice_in_dim(block, 0, width, axis=dim), axis, backward)
        block = jnp.concatenate([low, block, high], axis=dim)
    return block


def grid_factors(row_ids, lat_total):
    latitude = (-1.0 / 3.0 + 2.0 / 3.0 * (row_ids + 0.5) / lat_total) * jnp.pi
    return (1.0 / jnp.cos(latitude), jnp.sin(latitude))


def model_step(fields, orient, metric, coriolis):
    lon_wide = extended(fields, (("lon", 2),), 1)
    lat_wide = jnp.pad(fields, ((0, 0), (1, 1), (0, 0)))
    lon_diff = 0.5 * metric[:, None] * (lon_wide[:, :, 2:] - lon_wide[:, :, :-2])
    lat_diff = 0.5 * (lat_wide[:, 2:] - lat_wide[:, :-2])
    height, zonal, meridional = (fields[0], fields[1], fields[2])
    speed = orient * wave_speed
    turning = orient * rotation * coriolis[:, None]
    return jnp.stack(
        [
            height - speed * (lon_diff[1] + lat_diff[2]),
            zonal - speed * lon_diff[0] + turning * meridional,
            meridional - speed * lat_diff[0] - turning * zonal,
        ]
    )


def body(control, residual, direction, ens_perturb, localize, obs_cell, obs_slot, obs_weight):
    hi = lax.Precision.HIGHEST
    lat_total = localize.shape[0]
    tile_cols = control.shape[2]
    localized = jnp.einsum("ij,mjc->mic", localize, direction, precision=hi)
    increment = jnp.sum(ens_perturb.astype(jnp.float32) * localized[:, None], axis=0)
    lat_slab = lax.psum(increment, "ens")
    slab_rows = lat_slab.shape[1]
    cells = slab_rows * tile_cols
    row_ids = jnp.arange(slab_rows, dtype=jnp.int32).astype(jnp.float32)
    metric, coriolis = grid_factors(row_ids, lat_total)
    local_row = obs_cell // tile_cols
    inside = (local_row >= 0) & (local_row < slab_rows) & (obs_slot < STEPS)
    cell_index = jnp.clip(local_row, 0, slab_rows - 1) * tile_cols + obs_cell % tile_cols
    slot_index = obs_slot * cells + cell_index
    gather_index = jnp.clip(slot_index, 0, STEPS * cells - 1)
    tl_state = lat_slab
    heights = []
    for moment in range(STEPS):
        tl_state = model_step(tl_state, 1.0, metric, coriolis)
        heights.append(tl_state[0].reshape(-1))
    observed = jnp.concatenate(heights)[gather_index]
    weighted = jnp.where(inside, obs_weight * observed, 0.0)
    forcing = jnp.zeros(((STEPS + 1) * cells,), jnp.float32).at[slot_index].add(weighted)
    forcing = forcing.reshape(STEPS + 1, slab_rows, tile_cols)
    adjoint = jnp.zeros(lat_slab.shape, jnp.float32)
    for moment in reversed(range(STEPS)):
        adjoint = adjoint.at[0].add(forcing[moment])
        adjoint = model_step(adjoint, -1.0, metric, coriolis)
    projected = jnp.sum(ens_perturb.astype(jnp.float32) * adjoint[None], axis=1)
    pulled_back = jnp.einsum("ji,mjc->mic", localize, projected, precision=hi)
    image_vec = direction + pulled_back
    norm_old, curvature, cross_term, square = lax.psum(
        (
            jnp.sum(residual * residual),
            jnp.sum(direction * image_vec),
            jnp.sum(residual * image_vec),
            jnp.sum(image_vec * image_vec),
        ),
        ("ens", "lon"),
    )
    step_size = norm_old / curvature
    control_new = control + step_size * direction
    residual_new = residual - step_size * image_vec
    norm_new = norm_old - 2.0 * step_size * cross_term + step_size * step_size * square
    direction_new = residual_new + norm_new / norm_old * direction
    return (control_new, residual_new, direction_new)


def solution(mesh):
    in_specs = (
        P("ens", None, "lon"),
        P("ens", None, "lon"),
        P("ens", None, "lon"),
        P("ens", None, None, "lon"),
        P(),
        P("lon"),
        P("lon"),
        P("lon"),
    )
    out_specs = (P("ens", None, "lon"), P("ens", None, "lon"), P("ens", None, "lon"))
    return jax.shard_map(body, mesh=mesh, in_specs=in_specs, out_specs=out_specs, check_vma=False)
```

profile of v0, /device:TPU:12, one launch (start us, length us, event | category | flops | bytes accessed | tf_op | source)
XLA Modules:
  0.0 210.3 jit_solution(16358781422589472048)
XLA Ops:
  7.2 6.8 %fusion.6 = f32[2,1024,64]{1,2,0:T(8,128)S(1)} fusion(f32[2,1024,64]{1,2,0:T(8,128)} %param.16, f32[1024,1024]{1,0:T(8,128)} %param.18), kind=kOutput, calls=%fused_computation.10 | convolution fusion | flops 1610612736 | bytes 5242880 | tf_op jit(solution)/shard_map/ij,mjc->mic/dot_general | solution.py:51
  14.1 1.1 fusion.4
  15.3 49.7 %all-reduce.10.cloned.1.call-done = f32[3,1024,64]{1,2,0:T(8,128)} async-done(((f32[3,1024,64]{1,2,0:T(8,128)}), f32[3,1024,64]{1,2,0:T(8,128)}) %all-reduce.10.cloned.1.call-update) | async-done | bytes 786448 | tf_op jit(solution)/shard_map/psum | solution.py:53
  65.0 1.0 fusion.89
  66.1 0.5 collective-permute-start.1
  66.6 0.9 collective-permute-done
  67.5 1.8 collective-permute-done.1
  69.2 2.8 %fusion.34 = (f32[3,1024,64]{1,2,0:T(8,128)S(1)}, f32[3,1024,64]{1,2,0:T(8,128)S(1)}) fusion(f32[3,1024,64]{1,2,0:T(8,128)} %all-reduce.10.cloned.1.call-done, f32[3,1024,1]{1,2,0:T(1,128)S(1)} %collective-permute-done.1, f32[3,1024,1]{1,2,0:T(1,128)S(1)} %collective-permute-done, f32[1024]{0:T(1024)S(1)} %divide_multiply_fusion), kind=kLoop, calls=%fused_computation.57 | loop fusion | flops 1179648 | bytes 2387968 | tf_op jit(solution)/shard_map/mul | solution.py:33
  72.0 1.3 fusion.70
  73.4 0.8 collective-permute-start.2
  74.2 0.5 fusion.18
  74.7 0.2 copy.12
  75.1 0.6 collective-permute-done.2
  75.6 4.2 %collective-permute-done.3 = f32[3,1024,1]{1,2,0:T(1,128)S(1)} collective-permute-done((f32[3,1024,1]{1,2,0:T(1,128)S(1)}, f32[3,1024,1]{1,2,0:T(1,128)S(1)}, u32[]{:S(2)}, u32[]{:S(2)}) %collective-permute-start.3) | collective-permute-done | bytes 12320 | tf_op jit(solution)/shard_map/ppermute | solution.py:17
  79.9 0.2 fusion.32
  80.0 0.9 fusion.82
  81.1 0.5 collective-permute-start.5
  81.6 1.3 pad_slice_fusion.7
  82.9 1.1 copy.13
  84.2 1.8 collective-permute-done.5
  86.1 1.1 fusion.57
  87.1 0.2 copy.14
  87.6 23.0 %gather_fusion = f32[4096]{0:T(1024)S(1)} fusion(f32[196608]{0:T(1024)S(1)} %pad_maximum_fusion.16, s32[4096]{0:T(1024)S(1)} %get-tuple-element.53), kind=kCustom, calls=%fused_computation | custom fusion | bytes 49152 | tf_op jit(solution)/shard_map/gather | solution.py:68
  110.7 22.2 %scatter_custom_fusion = f32[262144]{0:T(1024)S(1)} fusion(s32[4096]{0:T(1024)S(1)} %compare_select_fusion.1, f32[4096]{0:T(1024)S(1)} %multiply_select_fusion, f32[]{:T(128)} %constant.120.clone.1), kind=kCustom, calls=%fused_computation.71 | custom fusion | flops 4096 | bytes 1048580 | tf_op jit(solution)/shard_map/scatter-add | solution.py:70
  132.9 0.1 slice.347
  133.1 0.2 copy.16
  133.3 1.3 collective-permute-start.6
  134.7 0.1 slice.357
  134.9 0.2 copy.17
  135.1 0.9 collective-permute-done.6
  136.0 2.3 %collective-permute-done.7 = f32[3,1024,1]{1,2,0:T(1,128)S(1)} collective-permute-done((f32[3,1024,1]{1,2,0:T(1,128)S(1)}, f32[3,1024,1]{1,2,0:T(1,128)S(1)}, u32[]{:S(2)}, u32[]{:S(2)}) %collective-permute-start.7) | collective-permute-done | bytes 12320 | tf_op jit(solution)/shard_map/ppermute | solution.py:17
  138.3 0.6 fusion.30
  139.2 0.6 collective-permute-start.8
  139.8 0.2 slice.370
  140.0 0.2 copy.18
  140.2 1.0 collective-permute-done.8
  141.2 4.2 %collective-permute-done.9 = f32[3,1024,1]{1,2,0:T(1,128)S(1)} collective-permute-done((f32[3,1024,1]{1,2,0:T(1,128)S(1)}, f32[3,1024,1]{1,2,0:T(1,128)S(1)}, u32[]{:S(2)}, u32[]{:S(2)}) %collective-permute-start.9) | collective-permute-done | bytes 12320 | tf_op jit(solution)/shard_map/ppermute | solution.py:17
  145.4 0.6 fusion.28
  146.0 0.2 fusion.46
  146.4 0.5 collective-permute-start.11
  146.9 0.9 collective-permute-done.10
  147.8 3.8 %collective-permute-done.11 = f32[3,1024,1]{1,2,0:T(1,128)S(1)} collective-permute-done((f32[3,1024,1]{1,2,0:T(1,128)S(1)}, f32[3,1024,1]{1,2,0:T(1,128)S(1)}, u32[]{:S(2)}, u32[]{:S(2)}) %collective-permute-start.11) | collective-permute-done | bytes 12320 | tf_op jit(solution)/shard_map/ppermute | solution.py:17
  151.5 0.6 fusion.26
  152.1 0.2 fusion.40
  152.4 0.2 fusion.5
  152.6 3.1 %multiply_reduce_fusion = (f32[]{:T(128)}, f32[]{:T(128)}, f32[]{:T(128)}, f32[]{:T(128)}, f32[2,1024,64]{1,2,0:T(8,128)S(1)}) fusion(f32[2,1024,64]{1,2,0:T(8,128)S(1)} %copy-done.3, f32[2,1024,64]{1,2,0:T(8,128)S(1)} %copy-done.1, f32[2,1024,64]{1,2,0:T(8,128)S(1)} %fusion.5, f32[1024,1024]{1,0:T(8,128)S(1)} %copy-done), kind=kOutput, calls=%fused_computation.66 | convolution fusion | flops 1611792384 | bytes 6291472 | tf_op jit(solution)/shard_map/ji,mjc->mic/dot_general | solution.py:77
  155.7 42.6 %all-reduce.7 = (f32[]{:T(128)}, f32[]{:T(128)}, f32[]{:T(128)}, f32[]{:T(128)}) all-reduce(f32[]{:T(128)} %get-tuple-element.41, f32[]{:T(128)} %get-tuple-element.42, f32[]{:T(128)} %get-tuple-element.40, f32[]{:T(128)} %get-tuple-element.39), channel_id=1, replica_groups=mesh['ens'=4,'lon'=8] {'ens','lon'}, use_global_device_ids=true, to_apply=%region_1.0 | all-reduce | flops 4 | bytes 32 | tf_op jit(solution)/shard_map/psum | solution.py:79
  202.2 1.3 multiply_add_fusion
  (52 shorter events, 1.8 us)
Async XLA Ops:
  7.2 6.9 %copy-start.2 = (bf16[2,3,1024,64]{2,3,1,0:T(8,128)(2,1)S(1)}, bf16[2,3,1024,64]{2,3,1,0:T(8,128)(2,1)}, u32[]{:S(2)}) copy-start(bf16[2,3,1024,64]{2,3,1,0:T(8,128)(2,1)} %param.17) | copy-start | bytes 2359300
  7.2 8.1 %copy-start.5 = (s32[4096]{0:T(1024)S(1)}, s32[4096]{0:T(1024)}, u32[]{:S(2)}) copy-start(s32[4096]{0:T(1024)} %param.19) | copy-start | bytes 49156
  7.2 8.1 %copy-start.6 = (s32[4096]{0:T(1024)S(1)}, s32[4096]{0:T(1024)}, u32[]{:S(2)}) copy-start(s32[4096]{0:T(1024)} %param.20) | copy-start | bytes 49156
  7.2 57.8 %all-reduce.10.cloned.1.call-start = ((), (), s32[]{:S(2)}) async-start(), calls=%async_computation | async-start | bytes 1572864 | tf_op jit(solution)/shard_map/psum | solution.py:53
  66.0 1.5 collective-permute-start
  66.1 3.2 %collective-permute-start.1 = (f32[3,1024,1]{1,2,0:T(1,128)S(1)}, f32[3,1024,1]{1,2,0:T(1,128)S(1)}, u32[]{:S(2)}, u32[]{:S(2)}) collective-permute-start(f32[3,1024,1]{1,2,0:T(1,128)S(1)} %get-tuple-element.95), channel_id=1, source_target_pairs={{0,1},{1,2},{2,3},{3,4},{4,5},{5,6},{6,7},{7,0},{8,9},{9,10},{10,1... | collective-permute-start | bytes 36872 | tf_op jit(solution)/shard_map/ppermute | solution.py:17
  73.4 2.2 %collective-permute-start.2 = (f32[3,1024,1]{1,2,0:T(1,128)S(1)}, f32[3,1024,1]{1,2,0:T(1,128)S(1)}, u32[]{:S(2)}, u32[]{:S(2)}) collective-permute-start(f32[3,1024,1]{1,2,0:T(1,128)S(1)} %get-tuple-element.90), channel_id=1, source_target_pairs={{1,0},{2,1},{3,2},{4,3},{5,4},{6,5},{7,6},{0,7},{9,8},{10,9},{11,1... | collective-permute-start | bytes 36872 | tf_op jit(solution)/shard_map/ppermute | solution.py:20
  74.2 5.6 %collective-permute-start.3 = (f32[3,1024,1]{1,2,0:T(1,128)S(1)}, f32[3,1024,1]{1,2,0:T(1,128)S(1)}, u32[]{:S(2)}, u32[]{:S(2)}) collective-permute-start(f32[3,1024,1]{1,2,0:T(1,128)S(1)} %get-tuple-element.91), channel_id=1, source_target_pairs={{0,1},{1,2},{2,3},{3,4},{4,5},{5,6},{6,7},{7,0},{8,9},{9,10},{10,1... | collective-permute-start | bytes 36872 | tf_op jit(solution)/shard_map/ppermute | solution.py:17
  81.0 3.2 %collective-permute-start.4 = (f32[3,1024,1]{1,2,0:T(1,128)S(1)}, f32[3,1024,1]{1,2,0:T(1,128)S(1)}, u32[]{:S(2)}, u32[]{:S(2)}) collective-permute-start(f32[3,1024,1]{1,2,0:T(1,128)S(1)} %get-tuple-element.85), channel_id=1, source_target_pairs={{1,0},{2,1},{3,2},{4,3},{5,4},{6,5},{7,6},{0,7},{9,8},{10,9},{11,1... | collective-permute-start | bytes 36872 | tf_op jit(solution)/shard_map/ppermute | solution.py:20
  81.1 5.0 %collective-permute-start.5 = (f32[3,1024,1]{1,2,0:T(1,128)S(1)}, f32[3,1024,1]{1,2,0:T(1,128)S(1)}, u32[]{:S(2)}, u32[]{:S(2)}) collective-permute-start(f32[3,1024,1]{1,2,0:T(1,128)S(1)} %get-tuple-element.84), channel_id=1, source_target_pairs={{0,1},{1,2},{2,3},{3,4},{4,5},{5,6},{6,7},{7,0},{8,9},{9,10},{10,1... | collective-permute-start | bytes 36872 | tf_op jit(solution)/shard_map/ppermute | solution.py:17
  87.6 23.1 %copy-start.7 = (f32[4096]{0:T(1024)S(1)}, f32[4096]{0:T(1024)}, u32[]{:S(2)}) copy-start(f32[4096]{0:T(1024)} %param.21) | copy-start | bytes 49156
  133.3 2.7 %collective-permute-start.6 = (f32[3,1024,1]{1,2,0:T(1,128)S(1)}, f32[3,1024,1]{1,2,0:T(1,128)S(1)}, u32[]{:S(2)}, u32[]{:S(2)}) collective-permute-start(f32[3,1024,1]{1,2,0:T(1,128)S(1)} %get-tuple-element.97), channel_id=1, source_target_pairs={{1,0},{2,1},{3,2},{4,3},{5,4},{6,5},{7,6},{0,7},{9,8},{10,9},{11,1... | collective-permute-start | bytes 36872 | tf_op jit(solution)/shard_map/ppermute | solution.py:20
  134.6 3.7 %collective-permute-start.7 = (f32[3,1024,1]{1,2,0:T(1,128)S(1)}, f32[3,1024,1]{1,2,0:T(1,128)S(1)}, u32[]{:S(2)}, u32[]{:S(2)}) collective-permute-start(f32[3,1024,1]{1,2,0:T(1,128)S(1)} %get-tuple-element.98), channel_id=1, source_target_pairs={{0,1},{1,2},{2,3},{3,4},{4,5},{5,6},{6,7},{7,0},{8,9},{9,10},{10,1... | collective-permute-start | bytes 36872 | tf_op jit(solution)/shard_map/ppermute | solution.py:17
  139.2 2.0 collective-permute-start.8
  139.8 5.6 %collective-permute-start.9 = (f32[3,1024,1]{1,2,0:T(1,128)S(1)}, f32[3,1024,1]{1,2,0:T(1,128)S(1)}, u32[]{:S(2)}, u32[]{:S(2)}) collective-permute-start(f32[3,1024,1]{1,2,0:T(1,128)S(1)} %get-tuple-element.78), channel_id=1, source_target_pairs={{0,1},{1,2},{2,3},{3,4},{4,5},{5,6},{6,7},{7,0},{8,9},{9,10},{10,1... | collective-permute-start | bytes 36872 | tf_op jit(solution)/shard_map/ppermute | solution.py:17
  146.3 1.5 collective-permute-start.10
  146.4 6.2 %copy-start = (f32[1024,1024]{1,0:T(8,128)S(1)}, f32[1024,1024]{1,0:T(8,128)}, u32[]{:S(2)}) copy-start(f32[1024,1024]{1,0:T(8,128)} %param.18) | copy-start | bytes 12582916
  146.4 6.2 %copy-start.1 = (f32[2,1024,64]{1,2,0:T(8,128)S(1)}, f32[2,1024,64]{1,2,0:T(8,128)}, u32[]{:S(2)}) copy-start(f32[2,1024,64]{1,2,0:T(8,128)} %param.16) | copy-start | bytes 1572868
  146.4 6.2 %copy-start.3 = (f32[2,1024,64]{1,2,0:T(8,128)S(1)}, f32[2,1024,64]{1,2,0:T(8,128)}, u32[]{:S(2)}) copy-start(f32[2,1024,64]{1,2,0:T(8,128)} %param.15) | copy-start | bytes 1572868
  146.4 5.1 %collective-permute-start.11 = (f32[3,1024,1]{1,2,0:T(1,128)S(1)}, f32[3,1024,1]{1,2,0:T(1,128)S(1)}, u32[]{:S(2)}, u32[]{:S(2)}) collective-permute-start(f32[3,1024,1]{1,2,0:T(1,128)S(1)} %get-tuple-element.74), channel_id=1, source_target_pairs={{0,1},{1,2},{2,3},{3,4},{4,5},{5,6},{6,7},{7,0},{8,9},{9,10},{10,1... | collective-permute-start | bytes 36872 | tf_op jit(solution)/shard_map/ppermute | solution.py:17
  152.3 49.9 %copy-start.4 = (f32[2,1024,64]{1,2,0:T(8,128)S(1)}, f32[2,1024,64]{1,2,0:T(8,128)}, u32[]{:S(2)}) copy-start(f32[2,1024,64]{1,2,0:T(8,128)} %param.14) | copy-start | bytes 1572868
Sparse Core Ops, SparseCore 0:
  15.3 49.6 all-reduce.9
where the time goes:
time: 211 us; the launch traced here: 210 us
  waiting for transfers between devices  72.1 us (34%)
  blocking collectives  42.6 us (20%)
  other arithmetic  34.3 us (16%)
  local copies, waits for them, and re-layouts  28.5 us (14%)
  between operations  18.5 us (9%)
  matrix products  9.88 us (5%)
  starting transfers between devices  4.47 us (2%)
    psum x1, waiting for transfers between devices, body(): lat_slab = lax.psum(increment, 'ens')  49.7 us
    psum x1, blocking collectives, body(): lax.psum((jnp.sum(residual * residual), jnp.sum(direction * image_vec), j...  42.6 us
    gather x1, local copies, waits for them, and re-layouts, body(): observed = jnp.concatenate(heights)[gather_index]  23 us
    scatter-add x1, other arithmetic, body(): jnp.zeros(((STEPS + 1) * cells,), jnp.float32).at[slot_index].add(weighted)  22.2 us
    ppermute x6, waiting for transfers between devices, extended(): lax.ppermute(lax.slice_in_dim(block, block.shape[dim] - width, None, axis...  18.1 us
    dot_general x1, matrix products, body(): localized = jnp.einsum('ij,mjc->mic', localize, direction, precision=hi)  6.79 us
    mul x6, other arithmetic, model_step(): 0.5 * metric[:, None] * (lon_wide[:, :, 2:] - lon_wide[:, :, :-2])  4.76 us
    ppermute x6, waiting for transfers between devices, extended(): lax.ppermute(lax.slice_in_dim(block, 0, width, axis=dim), axis, backward)  4.27 us
  transfers between devices with their start and end apart: 13, of which 12 were waited for; matrix products, arithmetic and copies ran while one was open for 2% of the time, Pallas kernels for 0%

commit v1 on v0

--- a/solution.py
+++ b/solution.py
@@ -50,7 +50,9 @@
     tile_cols = control.shape[2]
     localized = jnp.einsum("ij,mjc->mic", localize, direction, precision=hi)
     increment = jnp.sum(ens_perturb.astype(jnp.float32) * localized[:, None], axis=0)
-    lat_slab = lax.psum(increment, "ens")
+    lat_slab = increment
+    for hop in (1, 2):
+        lat_slab = lat_slab + lax.ppermute(lat_slab, "ens", [(dev, dev ^ hop) for dev in range(4)])
     slab_rows = lat_slab.shape[1]
     cells = slab_rows * tile_cols
     row_ids = jnp.arange(slab_rows, dtype=jnp.int32).astype(jnp.float32)

time: 211 us -> 180 us (0.85)
  waiting for transfers between devices: 72.1 us -> 56.8 us
  between operations: 18.5 us -> 5.1 us
  other arithmetic: 34.3 us -> 30.2 us
    psum x1 -> x0, waiting for transfers between devices: 49.7 us -> none  [body(): lat_slab = lax.psum(increment, 'ens')]
    ppermute x0 -> x2, waiting for transfers between devices: none -> 35.6 us  [body(): lax.ppermute(lat_slab, 'ens', [(dev, dev ^ hop) for dev in range(4)])]
    mul x6, other arithmetic: 4.76 us -> 2.55 us  [model_step(): 0.5 * metric[:, None] * (lon_wide[:, :, 2:] - lon_wide[:, :, :-2])]
    ppermute x0 -> x2, starting transfers between devices: none -> 2.12 us  [body(): lax.ppermute(lat_slab, 'ens', [(dev, dev ^ hop) for dev in range(4)])]
  transfers between devices with their start and end apart: 13 -> 14, of which waited for: 12 -> 13; matrix products, arithmetic and copies ran while one was open for 2% -> 2% of each run, Pallas kernels for 0% -> 0%
where the time goes in v1:
time: 180 us
  waiting for transfers between devices  56.8 us (32%)
  blocking collectives  43.5 us (24%)
  other arithmetic  30.2 us (17%)
  local copies, waits for them, and re-layouts  27.6 us (15%)
  matrix products  9.93 us (6%)
  starting transfers between devices  6.3 us (4%)
  between operations  5.1 us (3%)
    psum x1, blocking collectives, body(): lax.psum((jnp.sum(residual * residual), jnp.sum(direction * image_vec), j...  43.5 us
    ppermute x2, waiting for transfers between devices, body(): lax.ppermute(lat_slab, 'ens', [(dev, dev ^ hop) for dev in range(4)])  35.6 us
    gather x1, local copies, waits for them, and re-layouts, body(): observed = jnp.concatenate(heights)[gather_index]  23 us
    scatter-add x1, other arithmetic, body(): jnp.zeros(((STEPS + 1) * cells,), jnp.float32).at[slot_index].add(weighted)  22.2 us
    ppermute x6, waiting for transfers between devices, extended(): lax.ppermute(lax.slice_in_dim(block, block.shape[dim] - width, None, axis...  17.5 us
    dot_general x1, matrix products, body(): localized = jnp.einsum('ij,mjc->mic', localize, direction, precision=hi)  6.81 us
    ppermute x6, waiting for transfers between devices, extended(): lax.ppermute(lax.slice_in_dim(block, 0, width, axis=dim), axis, backward)  3.77 us
  transfers between devices with their start and end apart: 14, of which 13 were waited for; matrix products, arithmetic and copies ran while one was open for 2% of the time, Pallas kernels for 0%

profile of v1, /device:TPU:12, one launch (start us, length us, event | category | flops | bytes accessed | tf_op | source)
XLA Modules:
  0.0 179.5 jit_solution(17423917411397364370)
XLA Ops:
  0.7 6.8 %fusion.6 = f32[2,1024,64]{1,2,0:T(8,128)S(1)} fusion(f32[2,1024,64]{1,2,0:T(8,128)} %param.16, f32[1024,1024]{1,0:T(8,128)} %param.18), kind=kOutput, calls=%fused_computation.10 | convolution fusion | flops 1610612736 | bytes 5242880 | tf_op jit(solution)/shard_map/ij,mjc->mic/dot_general | solution.py:51
  7.5 0.2 fusion.4
  7.7 1.6 collective-permute-start
  9.2 17.8 %collective-permute-done = f32[3,1024,64]{1,2,0:T(8,128)S(1)} collective-permute-done((f32[3,1024,64]{1,2,0:T(8,128)S(1)}, f32[3,1024,64]{1,2,0:T(8,128)S(1)}, u32[]{:S(2)}, u32[]{:S(2)}) %collective-permute-start) | collective-permute-done | bytes 786464 | tf_op jit(solution)/shard_map/ppermute | solution.py:55
  27.1 0.6 collective-permute-start.1
  27.8 17.8 %collective-permute-done.1 = f32[3,1024,64]{1,2,0:T(8,128)S(1)} collective-permute-done((f32[3,1024,64]{1,2,0:T(8,128)S(1)}, f32[3,1024,64]{1,2,0:T(8,128)S(1)}, u32[]{:S(2)}, u32[]{:S(2)}) %collective-permute-start.1) | collective-permute-done | bytes 786464 | tf_op jit(solution)/shard_map/ppermute | solution.py:55
  45.8 0.5 collective-permute-start.3
  46.4 0.9 collective-permute-done.2
  47.2 1.8 collective-permute-done.3
  49.0 0.6 fusion.34
  49.6 0.2 fusion.70
  49.9 0.5 collective-permute-start.5
  50.4 0.5 fusion.18
  50.9 0.2 copy.12
  51.3 3.6 %collective-permute-done.5 = f32[3,1024,1]{1,2,0:T(1,128)S(1)} collective-permute-done((f32[3,1024,1]{1,2,0:T(1,128)S(1)}, f32[3,1024,1]{1,2,0:T(1,128)S(1)}, u32[]{:S(2)}, u32[]{:S(2)}) %collective-permute-start.5) | collective-permute-done | bytes 12320 | tf_op jit(solution)/shard_map/ppermute | solution.py:17
  54.9 0.2 fusion.32
  55.1 0.9 fusion.82
  56.1 0.5 collective-permute-start.7
  56.6 1.3 pad_slice_fusion.7
  58.0 1.1 copy.13
  59.3 1.9 %collective-permute-done.7 = f32[3,1024,1]{1,2,0:T(1,128)S(1)} collective-permute-done((f32[3,1024,1]{1,2,0:T(1,128)S(1)}, f32[3,1024,1]{1,2,0:T(1,128)S(1)}, u32[]{:S(2)}, u32[]{:S(2)}) %collective-permute-start.7) | collective-permute-done | bytes 12320 | tf_op jit(solution)/shard_map/ppermute | solution.py:17
  61.1 1.1 fusion.57
  62.2 0.2 copy.14
  62.7 23.0 %gather_fusion = f32[4096]{0:T(1024)S(1)} fusion(f32[196608]{0:T(1024)S(1)} %pad_maximum_fusion.16, s32[4096]{0:T(1024)S(1)} %get-tuple-element.53), kind=kCustom, calls=%fused_computation | custom fusion | bytes 49152 | tf_op jit(solution)/shard_map/gather | solution.py:70
  85.7 22.2 %scatter_custom_fusion = f32[262144]{0:T(1024)S(1)} fusion(s32[4096]{0:T(1024)S(1)} %compare_select_fusion.1, f32[4096]{0:T(1024)S(1)} %multiply_select_fusion, f32[]{:T(128)} %constant.120.clone.1), kind=kCustom, calls=%fused_computation.71 | custom fusion | flops 4096 | bytes 1048580 | tf_op jit(solution)/shard_map/scatter-add | solution.py:72
  108.1 0.2 copy.16
  108.3 1.3 collective-permute-start.8
  109.8 0.1 slice.357
  110.0 0.2 copy.17
  110.2 0.9 collective-permute-done.8
  111.1 2.3 %collective-permute-done.9 = f32[3,1024,1]{1,2,0:T(1,128)S(1)} collective-permute-done((f32[3,1024,1]{1,2,0:T(1,128)S(1)}, f32[3,1024,1]{1,2,0:T(1,128)S(1)}, u32[]{:S(2)}, u32[]{:S(2)}) %collective-permute-start.9) | collective-permute-done | bytes 12320 | tf_op jit(solution)/shard_map/ppermute | solution.py:17
  113.4 0.6 fusion.30
  114.2 0.6 collective-permute-start.10
  114.9 0.2 slice.370
  115.1 0.2 copy.18
  115.3 1.0 collective-permute-done.10
  116.3 4.2 %collective-permute-done.11 = f32[3,1024,1]{1,2,0:T(1,128)S(1)} collective-permute-done((f32[3,1024,1]{1,2,0:T(1,128)S(1)}, f32[3,1024,1]{1,2,0:T(1,128)S(1)}, u32[]{:S(2)}, u32[]{:S(2)}) %collective-permute-start.11) | collective-permute-done | bytes 12320 | tf_op jit(solution)/shard_map/ppermute | solution.py:17
  120.5 0.6 fusion.28
  121.1 0.2 fusion.46
  121.5 0.5 collective-permute-start.13
  122.0 0.9 collective-permute-done.12
  122.8 3.8 %collective-permute-done.13 = f32[3,1024,1]{1,2,0:T(1,128)S(1)} collective-permute-done((f32[3,1024,1]{1,2,0:T(1,128)S(1)}, f32[3,1024,1]{1,2,0:T(1,128)S(1)}, u32[]{:S(2)}, u32[]{:S(2)}) %collective-permute-start.13) | collective-permute-done | bytes 12320 | tf_op jit(solution)/shard_map/ppermute | solution.py:17
  126.6 0.6 fusion.26
  127.2 0.2 fusion.40
  127.4 0.2 fusion.5
  127.7 3.1 %multiply_reduce_fusion = (f32[]{:T(128)}, f32[]{:T(128)}, f32[]{:T(128)}, f32[]{:T(128)}, f32[2,1024,64]{1,2,0:T(8,128)S(1)}) fusion(f32[2,1024,64]{1,2,0:T(8,128)S(1)} %copy-done.3, f32[2,1024,64]{1,2,0:T(8,128)S(1)} %copy-done.1, f32[2,1024,64]{1,2,0:T(8,128)S(1)} %fusion.5, f32[1024,1024]{1,0:T(8,128)S(1)} %copy-done), kind=kOutput, calls=%fused_computation.66 | convolution fusion | flops 1611792384 | bytes 6291472 | tf_op jit(solution)/shard_map/ji,mjc->mic/dot_general | solution.py:79
  130.8 43.5 %all-reduce.7 = (f32[]{:T(128)}, f32[]{:T(128)}, f32[]{:T(128)}, f32[]{:T(128)}) all-reduce(f32[]{:T(128)} %get-tuple-element.41, f32[]{:T(128)} %get-tuple-element.42, f32[]{:T(128)} %get-tuple-element.40, f32[]{:T(128)} %get-tuple-element.39), channel_id=1, replica_groups=mesh['ens'=4,'lon'=8] {'ens','lon'}, use_global_device_ids=true, to_apply=%region_1.2 | all-reduce | flops 4 | bytes 32 | tf_op jit(solution)/shard_map/psum | solution.py:81
  178.2 1.3 multiply_add_fusion
  (55 shorter events, 2.2 us)
Async XLA Ops:
  0.6 6.8 %copy-start.2 = (bf16[2,3,1024,64]{2,3,1,0:T(8,128)(2,1)S(1)}, bf16[2,3,1024,64]{2,3,1,0:T(8,128)(2,1)}, u32[]{:S(2)}) copy-start(bf16[2,3,1024,64]{2,3,1,0:T(8,128)(2,1)} %param.17) | copy-start | bytes 2359300
  0.6 27.1 %copy-start.5 = (s32[4096]{0:T(1024)S(1)}, s32[4096]{0:T(1024)}, u32[]{:S(2)}) copy-start(s32[4096]{0:T(1024)} %param.19) | copy-start | bytes 49156
  0.7 27.1 %copy-start.6 = (s32[4096]{0:T(1024)S(1)}, s32[4096]{0:T(1024)}, u32[]{:S(2)}) copy-start(s32[4096]{0:T(1024)} %param.20) | copy-start | bytes 49156
  7.7 19.3 %collective-permute-start = (f32[3,1024,64]{1,2,0:T(8,128)S(1)}, f32[3,1024,64]{1,2,0:T(8,128)S(1)}, u32[]{:S(2)}, u32[]{:S(2)}) collective-permute-start(f32[3,1024,64]{1,2,0:T(8,128)S(1)} %fusion.4), channel_id=1, source_target_pairs={{0,8},{8,0},{16,24},{24,16},{1,9},{9,1},{17,25},{25,17},{2,10},{10... | collective-permute-start | bytes 2359304 | tf_op jit(solution)/shard_map/ppermute | solution.py:55
  27.1 18.5 %collective-permute-start.1 = (f32[3,1024,64]{1,2,0:T(8,128)S(1)}, f32[3,1024,64]{1,2,0:T(8,128)S(1)}, u32[]{:S(2)}, u32[]{:S(2)}) collective-permute-start(f32[3,1024,64]{1,2,0:T(8,128)S(1)} %add.242), channel_id=1, source_target_pairs={{0,16},{8,24},{16,0},{24,8},{1,17},{9,25},{17,1},{25,9},{2,18},{10... | collective-permute-start | bytes 2359304 | tf_op jit(solution)/shard_map/ppermute | solution.py:55
  45.7 1.5 collective-permute-start.2
  45.8 3.2 %collective-permute-start.3 = (f32[3,1024,1]{1,2,0:T(1,128)S(1)}, f32[3,1024,1]{1,2,0:T(1,128)S(1)}, u32[]{:S(2)}, u32[]{:S(2)}) collective-permute-start(f32[3,1024,1]{1,2,0:T(1,128)S(1)} %get-tuple-element.95), channel_id=1, source_target_pairs={{0,1},{1,2},{2,3},{3,4},{4,5},{5,6},{6,7},{7,0},{8,9},{9,10},{10,1... | collective-permute-start | bytes 36872 | tf_op jit(solution)/shard_map/ppermute | solution.py:17
  49.8 1.5 collective-permute-start.4
  49.9 5.0 %collective-permute-start.5 = (f32[3,1024,1]{1,2,0:T(1,128)S(1)}, f32[3,1024,1]{1,2,0:T(1,128)S(1)}, u32[]{:S(2)}, u32[]{:S(2)}) collective-permute-start(f32[3,1024,1]{1,2,0:T(1,128)S(1)} %get-tuple-element.91), channel_id=1, source_target_pairs={{0,1},{1,2},{2,3},{3,4},{4,5},{5,6},{6,7},{7,0},{8,9},{9,10},{10,1... | collective-permute-start | bytes 36872 | tf_op jit(solution)/shard_map/ppermute | solution.py:17
  56.1 3.2 %collective-permute-start.6 = (f32[3,1024,1]{1,2,0:T(1,128)S(1)}, f32[3,1024,1]{1,2,0:T(1,128)S(1)}, u32[]{:S(2)}, u32[]{:S(2)}) collective-permute-start(f32[3,1024,1]{1,2,0:T(1,128)S(1)} %get-tuple-element.85), channel_id=1, source_target_pairs={{1,0},{2,1},{3,2},{4,3},{5,4},{6,5},{7,6},{0,7},{9,8},{10,9},{11,1... | collective-permute-start | bytes 36872 | tf_op jit(solution)/shard_map/ppermute | solution.py:20
  56.1 5.0 %collective-permute-start.7 = (f32[3,1024,1]{1,2,0:T(1,128)S(1)}, f32[3,1024,1]{1,2,0:T(1,128)S(1)}, u32[]{:S(2)}, u32[]{:S(2)}) collective-permute-start(f32[3,1024,1]{1,2,0:T(1,128)S(1)} %get-tuple-element.84), channel_id=1, source_target_pairs={{0,1},{1,2},{2,3},{3,4},{4,5},{5,6},{6,7},{7,0},{8,9},{9,10},{10,1... | collective-permute-start | bytes 36872 | tf_op jit(solution)/shard_map/ppermute | solution.py:17
  62.7 23.1 %copy-start.7 = (f32[4096]{0:T(1024)S(1)}, f32[4096]{0:T(1024)}, u32[]{:S(2)}) copy-start(f32[4096]{0:T(1024)} %param.21) | copy-start | bytes 49156
  108.3 2.8 %collective-permute-start.8 = (f32[3,1024,1]{1,2,0:T(1,128)S(1)}, f32[3,1024,1]{1,2,0:T(1,128)S(1)}, u32[]{:S(2)}, u32[]{:S(2)}) collective-permute-start(f32[3,1024,1]{1,2,0:T(1,128)S(1)} %get-tuple-element.97), channel_id=1, source_target_pairs={{1,0},{2,1},{3,2},{4,3},{5,4},{6,5},{7,6},{0,7},{9,8},{10,9},{11,1... | collective-permute-start | bytes 36872 | tf_op jit(solution)/shard_map/ppermute | solution.py:20
  109.7 3.7 %collective-permute-start.9 = (f32[3,1024,1]{1,2,0:T(1,128)S(1)}, f32[3,1024,1]{1,2,0:T(1,128)S(1)}, u32[]{:S(2)}, u32[]{:S(2)}) collective-permute-start(f32[3,1024,1]{1,2,0:T(1,128)S(1)} %get-tuple-element.98), channel_id=1, source_target_pairs={{0,1},{1,2},{2,3},{3,4},{4,5},{5,6},{6,7},{7,0},{8,9},{9,10},{10,1... | collective-permute-start | bytes 36872 | tf_op jit(solution)/shard_map/ppermute | solution.py:17
  114.2 2.0 %collective-permute-start.10 = (f32[3,1024,1]{1,2,0:T(1,128)S(1)}, f32[3,1024,1]{1,2,0:T(1,128)S(1)}, u32[]{:S(2)}, u32[]{:S(2)}) collective-permute-start(f32[3,1024,1]{1,2,0:T(1,128)S(1)} %get-tuple-element.77), channel_id=1, source_target_pairs={{1,0},{2,1},{3,2},{4,3},{5,4},{6,5},{7,6},{0,7},{9,8},{10,9},{11,1... | collective-permute-start | bytes 36872 | tf_op jit(solution)/shard_map/ppermute | solution.py:20
  114.9 5.6 %collective-permute-start.11 = (f32[3,1024,1]{1,2,0:T(1,128)S(1)}, f32[3,1024,1]{1,2,0:T(1,128)S(1)}, u32[]{:S(2)}, u32[]{:S(2)}) collective-permute-start(f32[3,1024,1]{1,2,0:T(1,128)S(1)} %get-tuple-element.78), channel_id=1, source_target_pairs={{0,1},{1,2},{2,3},{3,4},{4,5},{5,6},{6,7},{7,0},{8,9},{9,10},{10,1... | collective-permute-start | bytes 36872 | tf_op jit(solution)/shard_map/ppermute | solution.py:17
  121.4 1.5 collective-permute-start.12
  121.4 6.2 %copy-start = (f32[1024,1024]{1,0:T(8,128)S(1)}, f32[1024,1024]{1,0:T(8,128)}, u32[]{:S(2)}) copy-start(f32[1024,1024]{1,0:T(8,128)} %param.18) | copy-start | bytes 12582916
  121.5 6.2 %copy-start.1 = (f32[2,1024,64]{1,2,0:T(8,128)S(1)}, f32[2,1024,64]{1,2,0:T(8,128)}, u32[]{:S(2)}) copy-start(f32[2,1024,64]{1,2,0:T(8,128)} %param.16) | copy-start | bytes 1572868
  121.5 6.2 %copy-start.3 = (f32[2,1024,64]{1,2,0:T(8,128)S(1)}, f32[2,1024,64]{1,2,0:T(8,128)}, u32[]{:S(2)}) copy-start(f32[2,1024,64]{1,2,0:T(8,128)} %param.15) | copy-start | bytes 1572868
  121.5 5.1 %collective-permute-start.13 = (f32[3,1024,1]{1,2,0:T(1,128)S(1)}, f32[3,1024,1]{1,2,0:T(1,128)S(1)}, u32[]{:S(2)}, u32[]{:S(2)}) collective-permute-start(f32[3,1024,1]{1,2,0:T(1,128)S(1)} %get-tuple-element.74), channel_id=1, source_target_pairs={{0,1},{1,2},{2,3},{3,4},{4,5},{5,6},{6,7},{7,0},{8,9},{9,10},{10,1... | collective-permute-start | bytes 36872 | tf_op jit(solution)/shard_map/ppermute | solution.py:17
  127.4 50.8 %copy-start.4 = (f32[2,1024,64]{1,2,0:T(8,128)S(1)}, f32[2,1024,64]{1,2,0:T(8,128)}, u32[]{:S(2)}) copy-start(f32[2,1024,64]{1,2,0:T(8,128)} %param.14) | copy-start | bytes 1572868
